TPU v7x, 32 devices: a whole 2x2x4 slice. The times are simulated.
32 devices in a mesh: seq: 8 (over z, y), grp: 4 (over x, core).
Axes of the slice: x: 2, y: 2, z: 4, core: 2. Of those that a mesh axis runs over, the one named last changes fastest.
Arguments:
- tokens: bfloat16 [4096, 2560], P('seq'), may hold values from -6 to 6
- norm_gain: float32 [2560], replicated, may hold values from 0.25 to 1.75
- inner_weight: bfloat16 [2560, 2, 5120], P(None, None, ('grp', 'seq')), may hold values from -0.125 to 0.125
- state_weight: bfloat16 [2560, 2, 128], replicated, may hold values from -0.125 to 0.125
- step_weight: bfloat16 [2560, 80], P(None, 'grp'), may hold values from -0.125 to 0.125
- step_bias: float32 [80], P('grp'), may hold values from -1 to 1
- decay_rate: float32 [80], P('grp'), may hold values from 4.8828124e-06 to 0.05
- skip_scale: float32 [80], P('grp'), may hold values from 0.5 to 1.5
- conv_inner: bfloat16 [4, 5120], P(None, 'grp'), may hold values from -3 to 3
- conv_state: bfloat16 [4, 2, 128], replicated, may hold values from -3 to 3
- out_gain: float32 [5120], P('grp'), may hold values from 0.25 to 1.75
- out_weight: bfloat16 [5120, 2560], P(None, 'grp'), may hold values from -0.078125 to 0.078125
Outputs:
- mixed: bfloat16 [4096, 2560], P('seq', 'grp')
All inputs are finite; a program needn't handle non-finite values.
Results may differ from a plain program's by a relative error of at most 0.0075.
Values may be sent and summed in bfloat16 or wider, within the bound.
No kernel may reach another device: no remote copies, remote signals or barrier semaphores. Data moves between devices by JAX's collectives and lax.ppermute only.
A program may use at most 64 MiB of HBM per device.

v0:
```python
from functools import partial
import jax
import jax.numpy as jnp
from jax import lax
from jax.sharding import PartitionSpec as P

SPAN = 256
EPS = 1e-05
HIGH = lax.Precision.HIGHEST


def from_behind(value, axis, steps):
    count = lax.axis_size(axis)
    leading, last = (max(0, -steps), min(count, count - steps))
    return lax.ppermute(value, axis, [(source, source + steps) for source in range(leading, last)])


def prefix(value, axis, combine, identity):
    length, place = (lax.axis_size(axis), lax.axis_index(axis))
    everything = jax.tree.map(lambda part: lax.all_gather(part, axis), value)
    start = jax.tree.map(
        lambda part, zero: jnp.broadcast_to(jnp.asarray(zero, part.dtype), part.shape),
        value,
        identity,
    )

    def step(k, before):
        reached = k < place
        new = combine(before, jax.tree.map(lambda part: part[k], everything))
        return jax.tree.map(lambda a, b: jnp.where(reached, a, b), new, before)

    return lax.fori_loop(0, length, step, start)


def conv_rows(before, current, weight):
    width = weight.shape[0]
    padded = jnp.concatenate([before, current], axis=0).astype(jnp.float32)
    length = current.shape[0]
    total = jnp.zeros(current.shape, jnp.float32)
    for offset in range(width):
        total = total + weight[offset].astype(jnp.float32) * padded[offset : offset + length]
    return jax.nn.silu(total).astype(jnp.bfloat16)


def span_step(rate, skip, state, inputs):
    xvals, bmat, cmat, delta = inputs
    logdec = -delta * rate[None, :]
    cumul = jnp.cumsum(logdec, axis=0)
    length = cumul.shape[0]
    scores = jnp.einsum("tn,sn->ts", cmat, bmat, preferred_element_type=jnp.float32)
    lower = jnp.arange(length)[:, None] >= jnp.arange(length)[None, :]
    diffs = cumul.T[:, :, None] - cumul.T[:, None, :]
    decay = jnp.exp(jnp.where(lower[None], diffs, -jnp.inf))
    mixer = (scores[None] * decay * delta.T[:, None, :]).astype(jnp.bfloat16)
    intra = jnp.einsum("hts,shp->thp", mixer, xvals, preferred_element_type=jnp.float32)
    inter = jnp.exp(cumul)[:, :, None] * jnp.einsum(
        "tn,hpn->thp", cmat.astype(jnp.float32), state, precision=HIGH
    )
    output = intra + inter + skip[None, :, None] * xvals.astype(jnp.float32)
    tail = jnp.exp(cumul[-1][None, :] - cumul) * delta
    weighted = (tail[:, :, None] * bmat.astype(jnp.float32)[:, None, :]).astype(jnp.bfloat16)
    update = jnp.einsum("shp,shn->hpn", xvals, weighted, preferred_element_type=jnp.float32)
    new_state = jnp.exp(cumul[-1])[:, None, None] * state + update
    return (new_state, output)


def body(
    tokens,
    norm_gain,
    inner_weight,
    state_weight,
    step_weight,
    step_bias,
    decay_rate,
    skip_scale,
    conv_inner,
    conv_state,
    out_gain,
    out_weight,
):
    tok_rows = tokens.shape[0]
    model_width = tokens.shape[1]
    wide = tokens.astype(jnp.float32)
    normed = (
        wide * lax.rsqrt(jnp.mean(wide * wide, axis=1, keepdims=True) + EPS) * norm_gain
    ).astype(jnp.bfloat16)
    piece = lax.all_gather(inner_weight, "seq", axis=2, tiled=True)
    count = piece.shape[2]
    flat = piece.reshape(piece.shape[0], 2 * count)
    result = jnp.dot(normed, flat, preferred_element_type=jnp.float32).astype(jnp.bfloat16)
    inner = result.reshape(tok_rows, 2, count)
    state_flat = state_weight.reshape(model_width, -1)
    state_pre = (
        jnp.dot(normed, state_flat, preferred_element_type=jnp.float32)
        .astype(jnp.bfloat16)
        .reshape(tok_rows, 2, -1)
    )
    delta = jax.nn.softplus(
        jnp.dot(normed, step_weight, preferred_element_type=jnp.float32) + step_bias
    )
    inner_values = inner[:, 0, :]
    width = conv_inner.shape[0]
    first_kept = tok_rows - width + 1
    before_values, before_state = from_behind(
        (inner_values[first_kept:], state_pre[first_kept:]), "seq", 1
    )
    values = conv_rows(before_values, inner_values, conv_inner)
    conv_out = conv_rows(before_state, state_pre, conv_state)
    heads_here = delta.shape[1]
    head_width = values.shape[1] // heads_here
    state_width = conv_out.shape[2]
    blocks = tok_rows // SPAN
    xs_blocks = values.reshape(blocks, SPAN, heads_here, head_width)
    b_blocks = conv_out[:, 0, :].reshape(blocks, SPAN, state_width)
    c_blocks = conv_out[:, 1, :].reshape(blocks, SPAN, state_width)
    d_blocks = delta.reshape(blocks, SPAN, heads_here)
    initial = jnp.zeros((heads_here, head_width, state_width), jnp.float32)
    final_state, outputs = lax.scan(
        partial(span_step, decay_rate, skip_scale),
        initial,
        (xs_blocks, b_blocks, c_blocks, d_blocks),
    )
    cumdev = jnp.cumsum(-delta * decay_rate[None, :], axis=0)
    totals = cumdev[-1]

    def combine(earlier, later):
        return (earlier[0] + later[0], jnp.exp(later[0])[:, None, None] * earlier[1] + later[1])

    scanned = prefix(
        (totals, final_state), "seq", combine, (jnp.zeros_like(totals), jnp.zeros_like(final_state))
    )
    incoming = scanned[1]
    cmat_wide = conv_out[:, 1, :].astype(jnp.float32)
    carried = jnp.exp(cumdev)[:, :, None] * jnp.einsum(
        "tn,hpn->thp", cmat_wide, incoming, precision=HIGH
    )
    mixed_heads = (outputs.reshape(tok_rows, heads_here, head_width) + carried).reshape(
        tok_rows, heads_here * head_width
    )
    gated = mixed_heads * jax.nn.silu(inner[:, 1, :].astype(jnp.float32))
    squares = lax.psum(jnp.sum(gated * gated, axis=1), "grp")
    row_scale = lax.rsqrt(squares / (lax.axis_size("grp") * gated.shape[1]) + EPS)
    scaled = (gated * out_gain).astype(jnp.bfloat16)
    summed = jnp.dot(
        lax.all_gather(scaled, "grp", axis=1, tiled=True),
        out_weight,
        preferred_element_type=jnp.float32,
    )
    return (summed * row_scale[:, None]).astype(jnp.bfloat16)


def solution(mesh):
    return jax.shard_map(
        body,
        mesh=mesh,
        in_specs=(
            P("seq", None),
            P(),
            P(None, None, ("grp", "seq")),
            P(),
            P(None, "grp"),
            P("grp"),
            P("grp"),
            P("grp"),
            P(None, "grp"),
            P(),
            P("grp"),
            P(None, "grp"),
        ),
        out_specs=P("seq", "grp"),
        check_vma=False,
    )
```

profile of v0, /device:TPU:0, one launch (start us, length us, event | category | flops | bytes accessed | tf_op | source)
XLA Modules:
  0.0 453.3 jit_solution(12982020083999643823)
XLA Ops:
  7.3 2.4 fusion.40
  9.8 0.9 fusion.56
  10.8 4.9 %collective-permute-start.1 = (bf16[3,2,128]{2,0,1:T(4,128)(2,1)S(1)}, bf16[3,2,128]{2,0,1:T(4,128)(2,1)S(1)}, u32[]{:S(2)}, u32[]{:S(2)}) collective-permute-start(bf16[3,2,128]{2,0,1:T(4,128)(2,1)S(1)} %slice_bitcast_fusion.2), channel_id=1, source_target_pairs={{0,4},{4,8},{8,12},{12,16},{16,20},{20,24},{24,28},{1,5},{5,9},{9,... | collective-permute-start | bytes 4616 | tf_op jit(solution)/shard_map/ppermute | solution.py:15
  16.4 1.5 compare_select_fusion.1
  18.1 1.0 maximum_convert_fusion.1
  20.8 174.0 %all-gather.6.cloned.1.call-done = bf16[2560,2,1280]{0,2,1:T(8,128)(2,1)} async-done(((bf16[2560,2,160]{0,2,1:T(8,128)(2,1)}), bf16[2560,2,1280]{0,2,1:T(8,128)(2,1)}) %all-gather.6.cloned.1.call-update) | async-done | bytes 13107216 | tf_op jit(solution)/shard_map/all_gather | solution.py:87
  194.8 11.2 %convolution_convert_fusion = bf16[512,2560]{1,0:T(8,128)(2,1)} fusion(bf16[2560,2560]{0,1:T(8,128)(2,1)} %bitcast.199, bf16[512,2560]{1,0:T(8,128)(2,1)S(1)} %copy-done.6, f32[2560]{0:T(1024)S(1)} %copy-done.16, f32[512]{0:T(512)S(1)} %add_rsqrt_fusion.1), kind=kOutput, calls=%fused_computation.59 | convolution fusion | flops 6717440000 | bytes 18362368 | tf_op jit(solution)/shard_map/dot_general | solution.py:90
  206.0 3.0 copy.65
  209.1 2.6 collective-permute-start
  211.8 2.0 slice_convert_fusion
  213.8 4.0 collective-permute-done
  217.8 0.7 maximum_convert_fusion
  218.5 3.2 multiply_convert_fusion.8
  222.4 71.2 %while.27 = (s32[]{:T(128)}, f32[20,64,128]{2,1,0:T(8,128)S(1)}, f32[2,256,20,64]{1,0,3,2:T(2,128)}, f32[2,256,20]{1,0,2:T(2,128)S(1)}, f32[20]{0:T(128)S(1)}, /...) while((s32[]{:T(128)}, f32[20,64,128]{2,1,0:T(8,128)S(1)}, ...), condition=%wide.region_4.5_spmd.clone, body=%wide.region_1.4_spmd.clone.sunk | while | flops 782684224 | bytes 15246184 | solution.py:118
  224.1 1.0 fusion.100
  225.2 1.5 fusion.101
  226.9 0.8 fusion.102
  227.7 1.3 copy.106
  229.1 27.0 %dynamic_update_slice.6 = f32[2,256,20,64]{1,0,3,2:T(2,128)} dynamic-update-slice(f32[2,256,20,64]{1,0,3,2:T(2,128)} %get-tuple-element.384, f32[1,256,20,64]{1,0,3,2:T(1,128)S(1)} %copy.106, s32[]{:T(128)} %get-tuple-element.382, s32[]{:T(128)} %constant.66.clone.1..sunk, s32[]{:T(128)} %constant.66.clone.1..sunk, s32[]{:T(128)} %constant.66.clone.1..sunk) | dynamic-update-slice | bytes 2621444 | tf_op jit(solution)/shard_map/while/body/jit(dynamic_update_index_in_dim)/dynamic_update_slice | solution.py:118
  256.1 0.9 bitcast_convert_fusion.6
  257.0 1.0 fusion.99
  259.7 1.0 fusion.100
  260.8 1.5 fusion.101
  262.5 0.8 fusion.102
  263.3 1.3 copy.106
  264.7 27.0 %dynamic_update_slice.6 = f32[2,256,20,64]{1,0,3,2:T(2,128)} dynamic-update-slice(f32[2,256,20,64]{1,0,3,2:T(2,128)} %get-tuple-element.384, f32[1,256,20,64]{1,0,3,2:T(1,128)S(1)} %copy.106, s32[]{:T(128)} %get-tuple-element.382, s32[]{:T(128)} %constant.66.clone.1..sunk, s32[]{:T(128)} %constant.66.clone.1..sunk, s32[]{:T(128)} %constant.66.clone.1..sunk) | dynamic-update-slice | bytes 2621444 | tf_op jit(solution)/shard_map/while/body/jit(dynamic_update_index_in_dim)/dynamic_update_slice | solution.py:118
  291.7 0.9 bitcast_convert_fusion.6
  292.6 1.0 fusion.99
  293.6 0.8 copy-done.2
  294.6 0.9 fusion.64
  295.5 1.2 reduce-window.16
  297.2 21.1 %all-gather.1 = f32[8,1,20]{2,1,0:T(1,128)S(1)} all-gather(f32[1,1,20]{2,1,0:T(1,128)S(1)} %bitcast.198), channel_id=1, replica_groups=mesh['seq'=8,'grp'=4] {'seq'}, dimensions={0}, use_global_device_ids=true | all-gather | bytes 720 | tf_op jit(solution)/shard_map/all_gather | solution.py:20
  318.3 4.9 %reshape.128 = f32[512,20,64]{0,2,1:T(8,128)} reshape(f32[2,256,20,64]{1,0,3,2:T(2,128)} %get-tuple-element.147) | data formatting | bytes 5242880 | tf_op jit(solution)/shard_map/reshape | solution.py:137
  323.2 59.1 %all-gather.10.cloned.1.call-done = f32[160,64,128]{2,1,0:T(8,128)} async-done(((f32[20,64,128]{2,1,0:T(8,128)}), f32[160,64,128]{2,1,0:T(8,128)}) %all-gather.10.cloned.1.call-update) | async-done | bytes 5242896 | tf_op jit(solution)/shard_map/all_gather | solution.py:20
  382.3 10.2 %while.28 = (s32[]{:T(128)}, f32[20,64,128]{2,1,0:T(8,128)S(1)}, s32[]{:T(128)}, f32[8,20]{1,0:T(8,128)S(1)}, f32[8,20,64,128]{3,2,1,0:T(8,128)}, /*index=5*/s32[]{:T(128)}, s32[]{:T(128)}) while((s32[]{:T(128)}, f32[20,64,128]{2,1,0:T(8,128)S(1)}, s32[]{:T(128)}, f32[8,20]{1,0:T(8,128)S(1)}, f32[8,20,64,128]{3,2,1,0:T(8,128)}, ...), condition=%wide.region_8.9_spmd.clone, body=%wide.region_7.8_spmd.clone.sunk | while | flops 655364 | bytes 1966425 | solution.py:32
  382.3 1.2 fusion.103
  383.5 1.2 fusion.103
  384.8 1.2 fusion.103
  386.1 1.2 fusion.103
  387.4 1.2 fusion.103
  388.6 1.2 fusion.103
  389.9 1.2 fusion.103
  391.2 1.2 fusion.103
  392.5 3.9 multiply_reduce_fusion
  396.4 2.0 fusion.51
  398.4 5.7 %psum.7 = f32[512]{0:T(512)S(1)} all-reduce(f32[512]{0:T(512)S(1)} %get-tuple-element.278), channel_id=1, replica_groups=mesh['seq'=8,'grp'=4] {'grp'}, use_global_device_ids=true, to_apply=%region_10.11 | all-reduce | flops 512 | bytes 4096 | tf_op jit(solution)/shard_map/psum | solution.py:141
  404.1 33.1 %all-gather.8.cloned.1.call-done = bf16[512,5120]{0,1:T(8,128)(2,1)} async-done(((bf16[512,1280]{0,1:T(8,128)(2,1)}), bf16[512,5120]{0,1:T(8,128)(2,1)}) %all-gather.8.cloned.1.call-update) | async-done | bytes 5242896 | tf_op jit(solution)/shard_map/all_gather | solution.py:145
  437.2 9.6 %fusion.52 = bf16[512,640]{1,0:T(8,128)(2,1)} fusion(bf16[512,5120]{0,1:T(8,128)(2,1)} %all-gather.8.cloned.1.call-done, bf16[5120,640]{1,0:T(8,128)(2,1)} %param.27, f32[512]{0:T(512)S(1)} %add_rsqrt_fusion), kind=kOutput, calls=%fused_computation.80 | convolution fusion | flops 3356098560 | bytes 12453888 | tf_op jit(solution)/shard_map/dot_general | solution.py:144
  (114 shorter events, 8.7 us)
Async XLA Ops:
  6.5 9.9 %copy-start = (bf16[2560,20]{0,1:T(8,128)(2,1)S(1)}, bf16[2560,20]{0,1:T(8,128)(2,1)}, u32[]{:S(2)}) copy-start(bf16[2560,20]{0,1:T(8,128)(2,1)} %param.20) | copy-start | bytes 307204
  6.5 3.2 copy-start.6
  6.5 3.2 copy-start.16
  6.5 188.2 %all-gather.6.cloned.1.call-start = ((), (), s32[]{:S(2)}) async-start(), calls=%async_computation | async-start | bytes 14745600 | tf_op jit(solution)/shard_map/all_gather | solution.py:87
  7.3 375.0 %all-gather.10.cloned.1.call-start = ((), (), s32[]{:S(2)}) async-start(), calls=%async_computation.2 | async-start | bytes 5898240 | tf_op jit(solution)/shard_map/all_gather | solution.py:20
  7.3 2.5 copy-start.15
  9.8 5.9 %copy-start.14 = (bf16[4,2,128]{2,1,0:T(2,128)(2,1)S(1)}, bf16[4,2,128]{2,1,0:T(2,128)(2,1)}, u32[]{:S(2)}) copy-start(bf16[4,2,128]{2,1,0:T(2,128)(2,1)} %param.25) | copy-start | bytes 6148
  9.8 6.6 %copy-start.17 = (f32[20]{0:T(128)S(1)}, f32[20]{0:T(128)}, u32[]{:S(2)}) copy-start(f32[20]{0:T(128)} %param.21) | copy-start | bytes 244
  10.8 7.3 %collective-permute-start.1 = (bf16[3,2,128]{2,0,1:T(4,128)(2,1)S(1)}, bf16[3,2,128]{2,0,1:T(4,128)(2,1)S(1)}, u32[]{:S(2)}, u32[]{:S(2)}) collective-permute-start(bf16[3,2,128]{2,0,1:T(4,128)(2,1)S(1)} %slice_bitcast_fusion.2), channel_id=1, source_target_pairs={{0,4},{4,8},{8,12},{12,16},{16,20},{20,24},{24,28},{1,5},{5,9},{9,... | collective-permute-start | bytes 4616 | tf_op jit(solution)/shard_map/ppermute | solution.py:15
  15.7 2.3 copy-start.10
  19.5 0.7 copy-start.7
  209.0 4.8 %copy-start.3 = (bf16[512,2560]{0,1:T(8,128)(2,1)}, bf16[512,2560]{0,1:T(8,128)(2,1)S(1)}, u32[]{:S(2)}) copy-start(bf16[512,2560]{0,1:T(8,128)(2,1)S(1)} %copy.65) | copy-start | bytes 7864324
  209.1 8.7 %collective-permute-start = (bf16[3,1280]{0,1:T(8,128)(2,1)S(1)}, bf16[3,1280]{0,1:T(8,128)(2,1)S(1)}, u32[]{:S(2)}, u32[]{:S(2)}) collective-permute-start(bf16[3,1280]{0,1:T(8,128)(2,1)S(1)} %slice_bitcast_fusion.1), channel_id=1, source_target_pairs={{0,4},{4,8},{8,12},{12,16},{16,20},{20,24},{24,28},{1,5},{5,9},{9,... | collective-permute-start | bytes 23048 | tf_op jit(solution)/shard_map/ppermute | solution.py:15
  221.8 0.7 copy-start.11
  221.8 0.7 copy-start.12
  222.4 0.6 copy-start.8
  229.1 28.9 %copy-start.9 = (f32[2,256,20]{1,0,2:T(2,128)S(1)}, f32[2,256,20]{1,0,2:T(2,128)}, u32[]{:S(2)}) copy-start(f32[2,256,20]{1,0,2:T(2,128)} %copy-done.8) | copy-start | bytes 122884 | tf_op jit(solution)/shard_map/while
  258.0 0.6 copy-start.8
  264.7 28.9 %copy-start.9 = (f32[2,256,20]{1,0,2:T(2,128)S(1)}, f32[2,256,20]{1,0,2:T(2,128)}, u32[]{:S(2)}) copy-start(f32[2,256,20]{1,0,2:T(2,128)} %copy-done.8) | copy-start | bytes 122884 | tf_op jit(solution)/shard_map/while
  293.6 0.8 copy-start.2
  294.5 142.7 %all-gather.8.cloned.1.call-start = ((), (), s32[]{:S(2)}) async-start(), calls=%async_computation.1 | async-start | bytes 6553600 | tf_op jit(solution)/shard_map/all_gather | solution.py:145
  318.3 74.2 %copy-start.5 = (f32[512,1,1280]{0,2,1:T(8,128)S(1)}, f32[512,1,1280]{0,2,1:T(8,128)}, u32[]{:S(2)}) copy-start(f32[512,1,1280]{0,2,1:T(8,128)} %get-tuple-element.268) | copy-start | bytes 7864324
  392.4 4.0 copy-start.4
  392.4 4.0 copy-start.13
  437.2 9.6 %copy-start.1 = (bf16[2560,20]{0,1:T(8,128)(2,1)S(1)}, bf16[2560,20]{0,1:T(8,128)(2,1)}, u32[]{:S(2)}) copy-start(bf16[2560,20]{0,1:T(8,128)(2,1)} %param.20) | copy-start | bytes 307204
Sparse Core Ops, SparseCore 0:
  9.5 185.2 all-gather.5
  294.6 87.5 all-gather.9
  398.5 38.5 all-gather.7
where the time goes:
time: 458 us; the launch traced here: 453 us
  waiting for transfers between devices  271 us (59%)
  local copies, waits for them, and re-layouts  71 us (16%)
  matrix products  35.7 us (8%)
  other arithmetic  27.3 us (6%)
  blocking collectives  26.8 us (6%)
  between operations  13.5 us (3%)
  starting transfers between devices  7.63 us (2%)
    all_gather x1, waiting for transfers between devices, body(): piece = lax.all_gather(inner_weight, 'seq', axis=2, tiled=True)  174 us
    all_gather x1, waiting for transfers between devices, prefix(): everything = jax.tree.map(lambda part: lax.all_gather(part, axis), value)  59.1 us
    dynamic_update_slice x4, local copies, waits for them, and re-layouts, body(): lax.scan(partial(span_step, decay_rate, skip_scale), initial, (xs_blocks,...  56.8 us
    all_gather x1, waiting for transfers between devices, body(): lax.all_gather(scaled, 'grp', axis=1, tiled=True)  33.1 us
    all_gather x1, blocking collectives, prefix(): everything = jax.tree.map(lambda part: lax.all_gather(part, axis), value)  21.1 us
    dot_general x1, matrix products, body(): jnp.dot(normed, flat, preferred_element_type=jnp.float32)  11.2 us
    select_n x8, other arithmetic, step(): return jax.tree.map(lambda a, b: jnp.where(reached, a, b), new, before)  9.86 us
    dot_general x1, matrix products, body(): jnp.dot(lax.all_gather(scaled, 'grp', axis=1, tiled=True), out_weight, pr...  9.57 us
  transfers between devices with their start and end apart: 5, of which 4 were waited for; matrix products, arithmetic and copies ran while one was open for 4% of the time, Pallas kernels for 0%

commit v1 on v0

--- a/solution.py
+++ b/solution.py
@@ -7,6 +7,17 @@
 SPAN = 256
 EPS = 1e-05
 HIGH = lax.Precision.HIGHEST
+
+
+def collect(value, axis, dim):
+    ways = lax.axis_size(axis)
+    pieces = [value]
+    for far in range(1, ways):
+        pieces.append(
+            lax.ppermute(pieces[far - 1], axis, [(d, (d - 1) % ways) for d in range(ways)])
+        )
+    line = jnp.concatenate(pieces, axis=dim)
+    return jnp.roll(line, lax.axis_index(axis) * value.shape[dim], axis=dim)
 
 
 def from_behind(value, axis, steps):
@@ -141,11 +152,7 @@
     squares = lax.psum(jnp.sum(gated * gated, axis=1), "grp")
     row_scale = lax.rsqrt(squares / (lax.axis_size("grp") * gated.shape[1]) + EPS)
     scaled = (gated * out_gain).astype(jnp.bfloat16)
-    summed = jnp.dot(
-        lax.all_gather(scaled, "grp", axis=1, tiled=True),
-        out_weight,
-        preferred_element_type=jnp.float32,
-    )
+    summed = jnp.dot(collect(scaled, "grp", 1), out_weight, preferred_element_type=jnp.float32)
     return (summed * row_scale[:, None]).astype(jnp.bfloat16)
 
 

time: 458 us -> 481 us (1.050)
  blocking collectives: 26.8 us -> 39.6 us
  local copies, waits for them, and re-layouts: 71 us -> 82.1 us
    all_gather x1 -> x0, waiting for transfers between devices: 33.1 us -> none  [body(): lax.all_gather(scaled, 'grp', axis=1, tiled=True)]
    ppermute x0 -> x3, waiting for transfers between devices: none -> 30.3 us  [collect(): lax.ppermute(pieces[far - 1], axis, [(d, (d - 1) % ways) for d in range(w...]
    psum x1, blocking collectives: 5.67 us -> 18.5 us  [body(): squares = lax.psum(jnp.sum(gated * gated, axis=1), 'grp')]
    unnamed x35 -> x49, local copies, waits for them, and re-layouts: 1.91 us -> 10.5 us
  transfers between devices with their start and end apart: 5 -> 7, of which waited for: 4 -> 5; matrix products, arithmetic and copies ran while one was open for 4% -> 4% of each run, Pallas kernels for 0% -> 0%
where the time goes in v1:
time: 481 us; the launch traced here: 477 us
  waiting for transfers between devices  268 us (56%)
  local copies, waits for them, and re-layouts  82.1 us (17%)
  blocking collectives  39.6 us (8%)
  matrix products  33.9 us (7%)
  other arithmetic  27.2 us (6%)
  between operations  13.8 us (3%)
  starting transfers between devices  11.4 us (2%)
    all_gather x1, waiting for transfers between devices, body(): piece = lax.all_gather(inner_weight, 'seq', axis=2, tiled=True)  174 us
    all_gather x1, waiting for transfers between devices, prefix(): everything = jax.tree.map(lambda part: lax.all_gather(part, axis), value)  59.1 us
    dynamic_update_slice x4, local copies, waits for them, and re-layouts, body(): lax.scan(partial(span_step, decay_rate, skip_scale), initial, (xs_blocks,...  56.8 us
    ppermute x3, waiting for transfers between devices, collect(): lax.ppermute(pieces[far - 1], axis, [(d, (d - 1) % ways) for d in range(w...  30.3 us
    all_gather x1, blocking collectives, prefix(): everything = jax.tree.map(lambda part: lax.all_gather(part, axis), value)  21.1 us
    psum x1, blocking collectives, body(): squares = lax.psum(jnp.sum(gated * gated, axis=1), 'grp')  18.5 us
    dot_general x1, matrix products, body(): jnp.dot(normed, flat, preferred_element_type=jnp.float32)  11.2 us
    unnamed x49, local copies, waits for them, and re-layouts  10.5 us
  transfers between devices with their start and end apart: 7, of which 5 were waited for; matrix products, arithmetic and copies ran while one was open for 4% of the time, Pallas kernels for 0%

profile of v1, /device:TPU:0, one launch (start us, length us, event | category | flops | bytes accessed | tf_op | source)
XLA Modules:
  0.0 476.5 jit_solution(15878481144771462428)
XLA Ops:
  7.3 2.4 fusion.40
  10.8 4.9 %collective-permute-start.1 = (bf16[3,2,128]{2,0,1:T(4,128)(2,1)S(1)}, bf16[3,2,128]{2,0,1:T(4,128)(2,1)S(1)}, u32[]{:S(2)}, u32[]{:S(2)}) collective-permute-start(bf16[3,2,128]{2,0,1:T(4,128)(2,1)S(1)} %slice_bitcast_fusion.2), channel_id=1, source_target_pairs={{0,4},{4,8},{8,12},{12,16},{16,20},{20,24},{24,28},{1,5},{5,9},{9,... | collective-permute-start | bytes 4616 | tf_op jit(solution)/shard_map/ppermute | solution.py:26
  16.4 1.5 compare_select_fusion.1
  20.8 173.9 %all-gather.5.cloned.1.call-done = bf16[2560,2,1280]{0,2,1:T(8,128)(2,1)} async-done(((bf16[2560,2,160]{0,2,1:T(8,128)(2,1)}), bf16[2560,2,1280]{0,2,1:T(8,128)(2,1)}) %all-gather.5.cloned.1.call-update) | async-done | bytes 13107216 | tf_op jit(solution)/shard_map/all_gather | solution.py:98
  194.8 11.2 %convolution_convert_fusion = bf16[512,2560]{1,0:T(8,128)(2,1)} fusion(bf16[2560,2560]{0,1:T(8,128)(2,1)} %bitcast.198, bf16[512,2560]{1,0:T(8,128)(2,1)S(1)} %copy-done.8, f32[2560]{0:T(1024)S(1)} %copy-done.18, f32[512]{0:T(512)S(1)} %add_rsqrt_fusion.1), kind=kOutput, calls=%fused_computation.61 | convolution fusion | flops 6717440000 | bytes 18362368 | tf_op jit(solution)/shard_map/dot_general | solution.py:101
  206.0 3.0 copy.65
  209.2 2.6 collective-permute-start
  211.8 2.0 slice_convert_fusion
  213.9 4.0 collective-permute-done
  218.6 3.2 multiply_convert_fusion.8
  222.5 71.1 %while.27 = (s32[]{:T(128)}, f32[20,64,128]{2,1,0:T(8,128)S(1)}, f32[2,256,20,64]{1,0,3,2:T(2,128)}, f32[2,256,20]{1,0,2:T(2,128)S(1)}, f32[20]{0:T(128)S(1)}, /...) while((s32[]{:T(128)}, f32[20,64,128]{2,1,0:T(8,128)S(1)}, ...), condition=%wide.region_4.5_spmd.clone, body=%wide.region_1.4_spmd.clone.sunk | while | flops 782684224 | bytes 15246703 | solution.py:129
  225.3 1.0 fusion.107
  226.4 1.5 fusion.108
  228.6 1.3 copy.106
  230.0 1.0 fusion.106
  231.0 27.1 %dynamic_update_slice.6 = f32[2,256,20,64]{1,0,3,2:T(2,128)} dynamic-update-slice(f32[2,256,20,64]{1,0,3,2:T(2,128)} %get-tuple-element.386, f32[1,256,20,64]{1,0,3,2:T(1,128)S(1)} %copy.106, s32[]{:T(128)S(6)} %copy.111, s32[]{:T(128)} %constant.85.clone.1..sunk, s32[]{:T(128)} %constant.85.clone.1..sunk, s32[]{:T(128)} %constant.85.clone.1..sunk) | dynamic-update-slice | bytes 2621444 | tf_op jit(solution)/shard_map/while/body/jit(dynamic_update_index_in_dim)/dynamic_update_slice | solution.py:129
  260.9 1.0 fusion.107
  261.9 1.5 fusion.108
  264.2 1.3 copy.106
  266.6 27.1 %dynamic_update_slice.6 = f32[2,256,20,64]{1,0,3,2:T(2,128)} dynamic-update-slice(f32[2,256,20,64]{1,0,3,2:T(2,128)} %get-tuple-element.386, f32[1,256,20,64]{1,0,3,2:T(1,128)S(1)} %copy.106, s32[]{:T(128)S(6)} %copy.111, s32[]{:T(128)} %constant.85.clone.1..sunk, s32[]{:T(128)} %constant.85.clone.1..sunk, s32[]{:T(128)} %constant.85.clone.1..sunk) | dynamic-update-slice | bytes 2621444 | tf_op jit(solution)/shard_map/while/body/jit(dynamic_update_index_in_dim)/dynamic_update_slice | solution.py:129
  295.4 1.2 reduce-window.16
  297.1 21.1 %all-gather.1 = f32[8,1,20]{2,1,0:T(1,128)S(1)} all-gather(f32[1,1,20]{2,1,0:T(1,128)S(1)} %bitcast.197), channel_id=1, replica_groups=mesh['seq'=8,'grp'=4] {'seq'}, dimensions={0}, use_global_device_ids=true | all-gather | bytes 720 | tf_op jit(solution)/shard_map/all_gather | solution.py:31
  318.2 4.9 %reshape.128 = f32[512,20,64]{0,2,1:T(8,128)} reshape(f32[2,256,20,64]{1,0,3,2:T(2,128)} %get-tuple-element.147) | data formatting | bytes 5242880 | tf_op jit(solution)/shard_map/reshape | solution.py:148
  323.2 59.1 %all-gather.7.cloned.1.call-done = f32[160,64,128]{2,1,0:T(8,128)} async-done(((f32[20,64,128]{2,1,0:T(8,128)}), f32[160,64,128]{2,1,0:T(8,128)}) %all-gather.7.cloned.1.call-update) | async-done | bytes 5242896 | tf_op jit(solution)/shard_map/all_gather | solution.py:31
  382.3 10.2 %while.28 = (s32[]{:T(128)}, f32[20,64,128]{2,1,0:T(8,128)S(1)}, s32[]{:T(128)}, f32[8,20]{1,0:T(8,128)S(1)}, f32[8,20,64,128]{3,2,1,0:T(8,128)}, /*index=5*/s32[]{:T(128)}, s32[]{:T(128)}) while((s32[]{:T(128)}, f32[20,64,128]{2,1,0:T(8,128)S(1)}, s32[]{:T(128)}, f32[8,20]{1,0:T(8,128)S(1)}, f32[8,20,64,128]{3,2,1,0:T(8,128)}, ...), condition=%wide.region_8.9_spmd.clone, body=%wide.region_7.8_spmd.clone.sunk | while | flops 655364 | bytes 1966433 | solution.py:43
  382.3 1.2 fusion.110
  383.6 1.2 fusion.110
  384.8 1.2 fusion.110
  386.1 1.2 fusion.110
  387.4 1.2 fusion.110
  388.7 1.2 fusion.110
  390.0 1.2 fusion.110
  391.2 1.2 fusion.110
  392.5 3.9 multiply_reduce_fusion
  396.5 1.9 constant_dynamic-update-slice_fusion.7
  398.4 15.1 %collective-permute-done.2 = bf16[512,1280]{0,1:T(8,128)(2,1)S(1)} collective-permute-done((bf16[512,1280]{0,1:T(8,128)(2,1)S(1)}, bf16[512,1280]{0,1:T(8,128)(2,1)S(1)}, u32[]{:S(2)}, u32[]{:S(2)}) %collective-permute-start.2) | collective-permute-done | bytes 1310752 | tf_op jit(solution)/shard_map/ppermute | solution.py:17
  413.5 1.9 collective-permute-start.3
  415.4 15.1 %collective-permute-done.3 = bf16[512,1280]{0,1:T(8,128)(2,1)S(1)} collective-permute-done((bf16[512,1280]{0,1:T(8,128)(2,1)S(1)}, bf16[512,1280]{0,1:T(8,128)(2,1)S(1)}, u32[]{:S(2)}, u32[]{:S(2)}) %collective-permute-start.3) | collective-permute-done | bytes 1310752 | tf_op jit(solution)/shard_map/ppermute | solution.py:17
  430.5 1.9 collective-permute-start.4
  432.4 18.5 %psum.7 = f32[512]{0:T(512)S(1)} all-reduce(f32[512]{0:T(512)S(1)} %get-tuple-element.280), channel_id=1, replica_groups=mesh['seq'=8,'grp'=4] {'grp'}, use_global_device_ids=true, to_apply=%region_10.11 | all-reduce | flops 512 | bytes 4096 | tf_op jit(solution)/shard_map/psum | solution.py:152
  450.9 1.2 constant_dynamic-update-slice_fusion.6
  452.1 1.2 constant_dynamic-update-slice_fusion.5
  453.3 2.6 constant_dynamic-update-slice_fusion.4
  455.9 1.2 constant_dynamic-update-slice_fusion.3
  457.1 1.1 constant_dynamic-update-slice_fusion.2
  458.3 1.2 constant_dynamic-update-slice_fusion.1
  459.5 2.5 constant_dynamic-update-slice_fusion
  462.0 7.7 %fusion.57 = bf16[512,640]{1,0:T(8,128)(2,1)} fusion(bf16[5120,640]{1,0:T(8,128)(2,1)S(1)} %bitcast.200, bf16[512,10240]{0,1:T(8,128)(2,1)} %constant_dynamic-update-slice_fusion, s32[]{:T(128)S(6)} %select_n.49, f32[512]{0:T(512)S(1)} %add_rsqrt_fusion), kind=kOutput, calls=%fused_computation.82 | convolution fusion | flops 3356098560 | bytes 12453892 | tf_op jit(solution)/shard_map/dot_general | solution.py:155
  (133 shorter events, 17.2 us)
Async XLA Ops:
  6.5 9.9 %copy-start = (bf16[2560,20]{0,1:T(8,128)(2,1)S(1)}, bf16[2560,20]{0,1:T(8,128)(2,1)}, u32[]{:S(2)}) copy-start(bf16[2560,20]{0,1:T(8,128)(2,1)} %param.20) | copy-start | bytes 307204
  6.5 3.2 copy-start.8
  6.5 3.2 copy-start.18
  6.5 188.2 %all-gather.5.cloned.1.call-start = ((), (), s32[]{:S(2)}) async-start(), calls=%async_computation | async-start | bytes 14745600 | tf_op jit(solution)/shard_map/all_gather | solution.py:98
  7.3 375.0 %all-gather.7.cloned.1.call-start = ((), (), s32[]{:S(2)}) async-start(), calls=%async_computation.1 | async-start | bytes 5898240 | tf_op jit(solution)/shard_map/all_gather | solution.py:31
  7.3 2.5 copy-start.17
  9.8 5.9 %copy-start.16 = (bf16[4,2,128]{2,1,0:T(2,128)(2,1)S(1)}, bf16[4,2,128]{2,1,0:T(2,128)(2,1)}, u32[]{:S(2)}) copy-start(bf16[4,2,128]{2,1,0:T(2,128)(2,1)} %param.25) | copy-start | bytes 6148
  9.8 6.6 %copy-start.19 = (f32[20]{0:T(128)S(1)}, f32[20]{0:T(128)}, u32[]{:S(2)}) copy-start(f32[20]{0:T(128)} %param.21) | copy-start | bytes 244
  10.8 7.3 %collective-permute-start.1 = (bf16[3,2,128]{2,0,1:T(4,128)(2,1)S(1)}, bf16[3,2,128]{2,0,1:T(4,128)(2,1)S(1)}, u32[]{:S(2)}, u32[]{:S(2)}) collective-permute-start(bf16[3,2,128]{2,0,1:T(4,128)(2,1)S(1)} %slice_bitcast_fusion.2), channel_id=1, source_target_pairs={{0,4},{4,8},{8,12},{12,16},{16,20},{20,24},{24,28},{1,5},{5,9},{9,... | collective-permute-start | bytes 4616 | tf_op jit(solution)/shard_map/ppermute | solution.py:26
  15.7 2.3 copy-start.12
  19.5 0.7 copy-start.9
  209.0 4.8 %copy-start.3 = (bf16[512,2560]{0,1:T(8,128)(2,1)}, bf16[512,2560]{0,1:T(8,128)(2,1)S(1)}, u32[]{:S(2)}) copy-start(bf16[512,2560]{0,1:T(8,128)(2,1)S(1)} %copy.65) | copy-start | bytes 7864324
  209.2 8.7 %collective-permute-start = (bf16[3,1280]{0,1:T(8,128)(2,1)S(1)}, bf16[3,1280]{0,1:T(8,128)(2,1)S(1)}, u32[]{:S(2)}, u32[]{:S(2)}) collective-permute-start(bf16[3,1280]{0,1:T(8,128)(2,1)S(1)} %slice_bitcast_fusion.1), channel_id=1, source_target_pairs={{0,4},{4,8},{8,12},{12,16},{16,20},{20,24},{24,28},{1,5},{5,9},{9,... | collective-permute-start | bytes 23048 | tf_op jit(solution)/shard_map/ppermute | solution.py:26
  221.8 0.7 copy-start.13
  221.8 0.7 copy-start.14
  222.5 0.6 copy-start.10
  230.0 28.1 %copy-start.11 = (f32[2,256,20]{1,0,2:T(2,128)S(1)}, f32[2,256,20]{1,0,2:T(2,128)}, u32[]{:S(2)}) copy-start(f32[2,256,20]{1,0,2:T(2,128)} %copy-done.10) | copy-start | bytes 122884 | tf_op jit(solution)/shard_map/while
  258.1 0.6 copy-start.10
  265.6 28.1 %copy-start.11 = (f32[2,256,20]{1,0,2:T(2,128)S(1)}, f32[2,256,20]{1,0,2:T(2,128)}, u32[]{:S(2)}) copy-start(f32[2,256,20]{1,0,2:T(2,128)} %copy-done.10) | copy-start | bytes 122884 | tf_op jit(solution)/shard_map/while
  293.7 0.8 copy-start.2
  318.2 74.2 %copy-start.7 = (f32[512,1,1280]{0,2,1:T(8,128)S(1)}, f32[512,1,1280]{0,2,1:T(8,128)}, u32[]{:S(2)}) copy-start(f32[512,1,1280]{0,2,1:T(8,128)} %get-tuple-element.268) | copy-start | bytes 7864324
  392.5 4.0 copy-start.4
  392.5 4.0 copy-start.15
  398.3 32.2 %copy-start.5 = (bf16[512,1280]{0,1:T(8,128)(2,1)}, bf16[512,1280]{0,1:T(8,128)(2,1)S(1)}, u32[]{:S(2)}) copy-start(bf16[512,1280]{0,1:T(8,128)(2,1)S(1)} %get-tuple-element.279) | copy-start | bytes 3932164
  398.3 15.1 %collective-permute-start.2 = (bf16[512,1280]{0,1:T(8,128)(2,1)S(1)}, bf16[512,1280]{0,1:T(8,128)(2,1)S(1)}, u32[]{:S(2)}, u32[]{:S(2)}) collective-permute-start(bf16[512,1280]{0,1:T(8,128)(2,1)S(1)} %get-tuple-element.279), channel_id=1, source_target_pairs={{0,3},{1,0},{2,1},{3,2},{4,7},{5,4},{6,5},{7,6},{8,11},{9,8},{10,9... | collective-permute-start | bytes 3932168 | tf_op jit(solution)/shard_map/ppermute | solution.py:17
  413.5 17.0 %collective-permute-start.3 = (bf16[512,1280]{0,1:T(8,128)(2,1)S(1)}, bf16[512,1280]{0,1:T(8,128)(2,1)S(1)}, u32[]{:S(2)}, u32[]{:S(2)}) collective-permute-start(bf16[512,1280]{0,1:T(8,128)(2,1)S(1)} %collective-permute-done.2), channel_id=1, source_target_pairs={{0,3},{1,0},{2,1},{3,2},{4,7},{5,4},{6,5},{7,6},{8,11},{9,8},{10,9... | collective-permute-start | bytes 3932168 | tf_op jit(solution)/shard_map/ppermute | solution.py:17
  430.5 22.8 %collective-permute-start.4 = (bf16[512,1280]{0,1:T(8,128)(2,1)S(1)}, bf16[512,1280]{0,1:T(8,128)(2,1)}, u32[]{:S(2)}, u32[]{:S(2)}) collective-permute-start(bf16[512,1280]{0,1:T(8,128)(2,1)S(1)} %collective-permute-done.3), channel_id=1, source_target_pairs={{0,3},{1,0},{2,1},{3,2},{4,7},{5,4},{6,5},{7,6},{8,11},{9,8},{10,9... | collective-permute-start | bytes 3932168 | tf_op jit(solution)/shard_map/ppermute | solution.py:17
  452.1 3.8 copy-start.6
  453.3 8.7 %slice-start = ((s8[6553600]{0:T(1024)(128)(4,1)}), s8[4194304]{0:T(1024)(128)(4,1)S(1)}, s32[]{:S(2)}) async-start(s8[6553600]{0:T(1024)(128)(4,1)} %bitcast.199), calls=%async_computation.2 | async-start | bytes 8388608
  457.1 4.8 %slice-start.1 = ((s8[6553600]{0:T(1024)(128)(4,1)}), s8[2359296]{0:T(1024)(128)(4,1)S(1)}, s32[]{:S(2)}) async-start(s8[6553600]{0:T(1024)(128)(4,1)} %bitcast.199), calls=%async_computation.3 | async-start | bytes 4718592
  462.0 7.7 %copy-start.1 = (bf16[2560,20]{0,1:T(8,128)(2,1)S(1)}, bf16[2560,20]{0,1:T(8,128)(2,1)}, u32[]{:S(2)}) copy-start(bf16[2560,20]{0,1:T(8,128)(2,1)} %param.20) | copy-start | bytes 307204
Sparse Core Ops, SparseCore 0:
  9.5 185.2 all-gather.4
  294.6 87.6 all-gather.6
